TPU v7x, 32 devices: a whole 2x2x4 slice. The times are simulated.
32 devices in a mesh: win: 32 (over z, y, x, core).
Axes of the slice: x: 2, y: 2, z: 4, core: 2. Of those that a mesh axis runs over, the one named last changes fastest.
Arguments:
- point_rows: int32 [64, 32768], P('win'), may hold values from 0 to 31
- point_cols: int32 [64, 32768], P('win'), may hold values from 0 to 1023
- point_chans: int32 [64, 32768], P('win'), may hold values from 0 to 3
- point_weights: bfloat16 [64, 32768], P('win'), may hold values from 0.25 to 4
- decay: float32 [64, 4], P('win'), may hold values from 0.3 to 1
Outputs:
- heat: float32 [64, 4, 32, 1024], P('win')
All inputs are finite; a program needn't handle non-finite values.
Results may differ from a plain program's by a relative error of at most 0.0003.
Values sent between devices are 32-bit elements; how exact they have to be, the bound alone decides.
A program may use at most 64 MiB of HBM per device.

v0:
```python
import functools

import jax
import jax.numpy as jnp
from jax import lax
from jax.experimental import pallas as pl
from jax.experimental.pallas import tpu as pltpu
from jax.sharding import PartitionSpec as P

IMAGE_LAYERS = 4
COLS = 1024
ROWS = 32
SLOTS = IMAGE_LAYERS * ROWS
LANES = 128
SUBLANES = 8
PART = 256
CHUNK = 512
POINTS = 16384
MESH = pl.DeviceIdType.MESH


def one_hot(index, size, on, points):
    spread = jnp.broadcast_to(index.astype(jnp.float32), (16, points)).astype(jnp.bfloat16)
    slots = lax.broadcasted_iota(jnp.int32, (16, points), 0).astype(jnp.float32).astype(jnp.bfloat16)
    off = jnp.zeros((16, points), jnp.bfloat16)
    return jnp.concatenate(
        [jnp.where(spread == slots + jnp.bfloat16(16.0 * g), on, off) for g in range(size // 16)], axis=0
    )


def bin_step(rows_ref, cols_ref, chans_ref, weights_ref, hist, window, chunk, first, points):
    here = pl.ds(pl.multiple_of(first, points), points)
    take = lambda ref: ref[window : window + 1, here]
    cols = take(cols_ref)
    cell = take(chans_ref) * ROWS + take(rows_ref) + ((cols >> 8) - chunk * (CHUNK // PART)) * SLOTS
    weights = jnp.broadcast_to(take(weights_ref).astype(jnp.float32), (16, points)).astype(jnp.bfloat16)
    right = one_hot(cols & (PART - 1), PART, weights, points)
    left = one_hot(cell, CHUNK // PART * SLOTS, jnp.ones((16, points), jnp.bfloat16), points)
    part = lax.dot_general(left, right, (((1,), (1,)), ((), ())), preferred_element_type=jnp.float32)
    for j in range(CHUNK // PART):
        hist[window, chunk, :, j * PART : (j + 1) * PART] += part[j * SLOTS : (j + 1) * SLOTS]


def across(tile, width):
    return jnp.concatenate([tile] * (width // LANES), axis=1)


def kernel(
    n, size, points,
    rows_hbm, cols_hbm, chans_hbm, weights_hbm, decay_ref, out_hbm,
    rows_ref, cols_ref, chans_ref, weights_ref, hist, stage, inbox, total, earlier, carried, spread, back, prefix,
    load_sem, store_sem, go_send, go_recv, up_send, up_recv, back_send, back_recv,
):
    windows, count = rows_ref.shape
    groups = n // size
    piece = SLOTS // size
    chunks = COLS // CHUNK
    me = lax.axis_index("win")
    group, member = lax.div(me, size), lax.rem(me, size)
    mate = lambda k: group * size + lax.rem(member + k, size)

    sources = ((cols_hbm, cols_ref), (chans_hbm, chans_ref), (rows_hbm, rows_ref), (weights_hbm, weights_ref))
    loads = [
        pltpu.make_async_copy(source, target, load_sem.at[i]) for i, (source, target) in enumerate(sources)
    ]
    for load in loads:
        load.start()

    barrier = pltpu.get_barrier_semaphore()
    for k in range(1, size):
        pl.semaphore_signal(barrier, inc=1, device_id=(mate(k),), device_id_type=MESH)
    for k in range(1, groups):
        pl.semaphore_signal(barrier, inc=1, device_id=(lax.rem(me + k * size, n),), device_id_type=MESH)

    hist[...] = jnp.zeros(hist.shape, jnp.float32)
    for load in loads:
        load.wait()

    def sent(ref, chunk):
        return ref if chunk == 0 else ref.at[:, pl.ds(0, CHUNK)]

    def go(chunk, k):
        peer = lax.rem(member + k, size)
        return pltpu.make_async_remote_copy(
            src_ref=sent(stage.at[chunk, peer], chunk), dst_ref=sent(inbox.at[chunk, member], chunk),
            send_sem=go_send.at[chunk, k], recv_sem=go_recv.at[chunk, member],
            device_id=(mate(k),), device_id_type=MESH,
        )

    def come(chunk, k):
        peer = lax.rem(member + k, size)
        return pltpu.make_async_remote_copy(
            src_ref=sent(stage.at[chunk, peer], chunk), dst_ref=sent(inbox.at[chunk, peer], chunk),
            send_sem=go_send.at[chunk, k], recv_sem=go_recv.at[chunk, peer],
            device_id=(mate(k),), device_id_type=MESH,
        )

    def up(chunk, k, slot):
        return pltpu.make_async_remote_copy(
            src_ref=sent(total.at[chunk], chunk), dst_ref=sent(earlier.at[chunk, slot], chunk),
            send_sem=up_send.at[chunk, k], recv_sem=up_recv.at[chunk, slot],
            device_id=(lax.rem(me + k * size, n),), device_id_type=MESH,
        )

    def give(chunk, k):
        peer = lax.rem(member + k, size)
        return pltpu.make_async_remote_copy(
            src_ref=back.at[chunk, peer], dst_ref=prefix.at[chunk, member],
            send_sem=back_send.at[chunk, k], recv_sem=back_recv.at[chunk, member],
            device_id=(mate(k),), device_id_type=MESH,
        )

    def get(chunk, k):
        peer = lax.rem(member + k, size)
        return pltpu.make_async_remote_copy(
            src_ref=back.at[chunk, peer], dst_ref=prefix.at[chunk, peer],
            send_sem=back_send.at[chunk, k], recv_sem=back_recv.at[chunk, peer],
            device_id=(mate(k),), device_id_type=MESH,
        )

    def send_sums(chunk):
        for p in range(size):
            channel = p * piece // ROWS
            at = slice(p * piece, (p + 1) * piece)
            running = hist[0, chunk, at, :]
            factor = jnp.full((piece, LANES), decay_ref[0, channel], jnp.float32)
            for window in range(1, windows):
                running = decay_ref[window, channel] * running + hist[window, chunk, at, :]
                factor = factor * decay_ref[window, channel]
            stage[chunk, p, :, :CHUNK] = running
            if chunk == 0:
                stage[chunk, p, :, CHUNK:] = factor
        if chunk == 0:
            pl.semaphore_wait(barrier, size - 1 + groups - 1)
        for k in range(1, size):
            go(chunk, k).start()
        wide = CHUNK if chunk else CHUNK + LANES
        inbox[chunk, member, :, :wide] = stage[chunk, member, :, :wide]

    def scan_group(chunk):
        for k in range(1, size):
            come(chunk, k).wait_recv()
        running = jnp.zeros((piece, CHUNK), jnp.float32)
        factor = jnp.ones((piece, LANES), jnp.float32)
        for m in range(size):
            back[chunk, m] = running
            by = inbox[0, m, :, CHUNK:]
            if chunk == 0:
                spread[m] = factor
            running = across(by, CHUNK) * running + inbox[chunk, m, :, :CHUNK]
            if chunk == 0:
                factor = factor * by
        total[chunk, :, :CHUNK] = running
        if chunk == 0:
            total[chunk, :, CHUNK:] = factor
        for k in range(1, groups):

            @pl.when(group + k < groups)
            def _():
                up(chunk, k, group).start()

    def send_back(chunk):
        if groups > 1:
            carried[...] = jnp.zeros((piece, CHUNK), jnp.float32)
            for g in range(groups - 1):

                @pl.when(g < group)
                def _():
                    up(chunk, 1, g).wait_recv()
                    by = earlier[0, g, :, CHUNK:]
                    carried[...] = across(by, CHUNK) * carried[...] + earlier[chunk, g, :, :CHUNK]

            @pl.when(group > 0)
            def _():
                before = carried[...]
                for m in range(size):
                    back[chunk, m] += across(spread[m], CHUNK) * before

        for k in range(1, size):
            give(chunk, k).start()
        prefix[chunk, member] = back[chunk, member]

    def store(chunk, window):
        return pltpu.make_async_copy(
            hist.at[window, chunk],
            out_hbm.at[window, :, pl.ds(chunk * CHUNK, CHUNK)],
            store_sem.at[chunk, window],
        )

    def finish(chunk):
        for k in range(1, size):
            get(chunk, k).wait_recv()
        for p in range(size):
            channel = p * piece // ROWS
            at = slice(p * piece, (p + 1) * piece)
            running = prefix[chunk, p]
            for window in range(windows):
                running = decay_ref[window, channel] * running + hist[window, chunk, at, :]
                hist[window, chunk, at, :] = running
        for window in range(windows):
            store(chunk, window).start()

    steps = count // points
    for chunk in range(chunks):
        for window in range(windows):

            if chunk > 0 and window == windows - 1:
                scan_group(chunk - 1)

            def step(i, carry):
                if chunk > 0 and window == windows - 1 and steps > 1:

                    @pl.when(i == steps - 1)
                    def _():
                        send_back(chunk - 1)

                bin_step(
                    rows_ref, cols_ref, chans_ref, weights_ref, hist, window, chunk, i * points, points
                )
                return carry

            lax.fori_loop(0, steps, step, 0)
        send_sums(chunk)
        if chunk > 0:
            if steps == 1:
                send_back(chunk - 1)
            finish(chunk - 1)
    scan_group(chunks - 1)
    send_back(chunks - 1)
    finish(chunks - 1)

    for chunk in range(chunks):
        for window in range(windows):
            store(chunk, window).wait()
        for k in range(1, size):
            go(chunk, k).wait_send()
            give(chunk, k).wait_send()
        for k in range(1, groups):

            @pl.when(group + k < groups)
            def _():
                up(chunk, k, group).wait_send()


def local(n, point_rows, point_cols, point_chans, point_weights, decay):
    windows, count = point_rows.shape
    size = max(s for s in range(1, SLOTS // SUBLANES + 1) if n % s == 0 and SLOTS % (s * SUBLANES) == 0)
    groups = n // size
    piece, chunks = SLOTS // size, COLS // CHUNK
    wide = CHUNK + LANES
    dma = pltpu.SemaphoreType.DMA
    heat = pl.pallas_call(
        functools.partial(kernel, n, size, min(POINTS, count)),
        out_shape=jax.ShapeDtypeStruct((windows, SLOTS, COLS), jnp.float32),
        in_specs=[pl.BlockSpec(memory_space=pl.ANY)] * 4 + [pl.BlockSpec(memory_space=pltpu.SMEM)],
        out_specs=pl.BlockSpec(memory_space=pl.ANY),
        scratch_shapes=[
            pltpu.VMEM((windows, count), jnp.int32),
            pltpu.VMEM((windows, count), jnp.int32),
            pltpu.VMEM((windows, count), jnp.int32),
            pltpu.VMEM((windows, count), jnp.bfloat16),
            pltpu.VMEM((windows, chunks, SLOTS, CHUNK), jnp.float32),
            pltpu.VMEM((chunks, size, piece, wide), jnp.float32),
            pltpu.VMEM((chunks, size, piece, wide), jnp.float32),
            pltpu.VMEM((chunks, piece, wide), jnp.float32),
            pltpu.VMEM((chunks, groups, piece, wide), jnp.float32),
            pltpu.VMEM((piece, CHUNK), jnp.float32),
            pltpu.VMEM((size, piece, LANES), jnp.float32),
            pltpu.VMEM((chunks, size, piece, CHUNK), jnp.float32),
            pltpu.VMEM((chunks, size, piece, CHUNK), jnp.float32),
            dma((4,)),
            dma((chunks, windows)),
            dma((chunks, size)),
            dma((chunks, size)),
            dma((chunks, groups)),
            dma((chunks, groups)),
            dma((chunks, size)),
            dma((chunks, size)),
        ],
        compiler_params=pltpu.CompilerParams(
            collective_id=0, has_side_effects=True, vmem_limit_bytes=56 * 2**20
        ),
    )(point_rows, point_cols, point_chans, point_weights, decay)
    return heat.reshape(windows, IMAGE_LAYERS, ROWS, COLS)


def solution(mesh):
    placed = (P("win", None), P("win", None), P("win", None), P("win", None), P("win", None))
    return jax.shard_map(
        functools.partial(local, mesh.shape["win"]),
        mesh=mesh, in_specs=placed, out_specs=P("win", None, None, None), check_vma=False,
    )
```

profile of v0, /device:TPU:17, one launch (start us, length us, event | category | flops | bytes accessed | tf_op | source)
XLA Modules:
  0.0 39.0 jit_solution(1973150594432166078)
XLA Ops:
  0.0 36.7 %shard_map.55 = f32[2,128,1024]{2,1,0:T(8,128)} custom-call(s32[2,32768]{1,0:T(2,128)} %rows_hbm.1, s32[2,32768]{1,0:T(2,128)} %cols_hbm.1, s32[2,32768]{1,0:T(2,128)} %chans_hbm.1, bf16[2,32768]{1,0:T(2,128)(2,1)} %weights_hbm.1, f32[2,4]{1,0:T(2,128)} %decay_ref.1), custom_call_target="tpu_custom_call" | custom-call | tf_op jit(solution)/shard_map/pallas_call | solution.py:252
  36.7 2.3 %copy.7 = f32[2,4,32,1024]{3,2,1,0:T(8,128)} copy(f32[2,4,32,1024]{3,2,1,0:T(8,128)} %bitcast.1) | data formatting | bytes 2097152
where the time goes:
time: 39.2 us; the launch traced here: 39 us
  Pallas kernels  36.7 us (94%)
  local copies, waits for them, and re-layouts  2.31 us (6%)
    pallas_call x1, Pallas kernels, local(): pl.pallas_call(functools.partial(kernel, n, size, min(POINTS, count)), ou...  36.7 us
    unnamed x1, local copies, waits for them, and re-layouts  2.31 us

commit v1 on v0

v1 whole, which is shorter than its diff:
```python
import functools
import jax, jax.numpy as jnp
from jax import lax
from jax.experimental import pallas as pl
from jax.experimental.pallas import tpu as pltpu
from jax.sharding import PartitionSpec as P
IMAGE_LAYERS=4
SLOTS=128; ROWS=32; COLS=1024; PART=256; LANES=128; SUB=8
PARTS=2
UNROLL=8
def hot(index, on):
    spread = jnp.broadcast_to(index, (16, LANES)).astype(jnp.bfloat16)
    slots = lax.broadcasted_iota(jnp.int32, (16, LANES), 0).astype(jnp.float32).astype(jnp.bfloat16)
    off = jnp.zeros((16, LANES), jnp.bfloat16)
    return jnp.concatenate([jnp.where(spread == slots + jnp.bfloat16(16.0*g), on, off) for g in range(16)], axis=0)

def swap(x, bits):
    sub = lax.broadcasted_iota(jnp.int32, (SUB, LANES), 0)
    return jnp.take_along_axis(x, sub ^ bits, axis=0)

def exchange(xs, i, j):
    xs[i], xs[j] = jnp.minimum(xs[i], xs[j]), jnp.maximum(xs[i], xs[j])

def sort_rows(xs):
    n=len(xs); xs=list(xs)
    sub = lax.broadcasted_iota(jnp.int32, (SUB, LANES), 0)
    k=2
    while k<=n:
        for b in range(0,n,k):
            for t in range(k//2): exchange(xs,b+t,b+k-1-t)
        d=k//4
        while d:
            for i in range(n):
                if not i & d: exchange(xs,i,i+d)
            d//=2
        k*=2
    width=1
    while width<SUB:
        low = (sub & width)==0
        ys=[swap(x,2*width-1) for x in xs]
        xs=[jnp.where(low,jnp.minimum(xs[i],ys[n-1-i]),jnp.maximum(xs[i],ys[n-1-i])) for i in range(n)]
        d=width//2
        while d:
            low=(sub & d)==0
            xs=[jnp.where(low,jnp.minimum(x,y),jnp.maximum(x,y)) for x,y in ((x,swap(x,d)) for x in xs)]
            d//=2
        d=n//2
        while d:
            for i in range(n):
                if not i & d: exchange(xs,i,i+d)
            d//=2
        width*=2
    return xs

def kernel(rows_hbm, cols_hbm, chans_hbm, weights_hbm, decay_hbm, out, fact, rows, cols, chans, weights, decay, keys, place, where_, weigh, sem):
    copies=[pltpu.make_async_copy(a,b,sem.at[i]) for i,(a,b) in enumerate(((decay_hbm,decay),(weights_hbm,weights),(cols_hbm,cols),(chans_hbm,chans),(rows_hbm,rows)))]
    for copy in copies: copy.start()
    for copy in copies: copy.wait()
    pl.run_scoped(functools.partial(bin_points,rows,cols,chans,weights,decay,out,fact,keys,place,where_,weigh),
        pltpu.ACC(0)((256,256),jnp.float32),pltpu.ACC(1)((256,256),jnp.float32))

def bin_points(rows, cols, chans, weights, decay, out, fact, keys, place, where_, weigh, *accs):
    windows = out.shape[0]
    for channel in range(IMAGE_LAYERS):
        factor = jnp.float32(1.0)
        for w in range(windows):
            factor = factor * decay[w, channel]
            fact[w, channel : channel + 1, :] = jnp.full((1, LANES), factor, jnp.float32)
    total = rows.shape[0]; height = total//windows
    for a in accs: out[0,:,0:256]=pltpu.matmul_pop(a)[:128]
    for v in range(total//16):
        at=pl.ds(16*v,16)
        c=cols[at,:]; k=chans[at,:]
        w=(weights[at,:].astype(jnp.float32)*512.0).astype(jnp.int32)
        lidx=((k>>1)<<8)|((c>>8)<<6)|((k&1)<<5)|rows[at,:]
        keys[at,:]=(lidx<<20)|((c&255)<<12)|w
    bounds=[]
    n=height//SUB
    for w in range(windows):
        xs=[keys[pl.ds(w+windows*SUB*v,SUB,stride=windows),:] for v in range(n)]
        xs=sort_rows(xs)
        first=jnp.zeros((SUB,LANES),jnp.int32)
        for v in range(n):
            x=xs[v]
            first=first+jnp.where(x<(1<<28),1,0)
            at=pl.ds(v,SUB,stride=n)
            place[w,at,:]=(x>>20).astype(jnp.float32)
            where_[w,at,:]=((x>>12)&255).astype(jnp.float32)
            weigh[w,at,:]=(x&4095).astype(jnp.float32)*(1.0/512.0)
        first=jnp.sum(first,axis=0,keepdims=True)
        bounds.append((jnp.min(first),jnp.max(first)))
    one=jnp.ones((16,LANES),jnp.bfloat16)
    step=2*UNROLL
    def right(w,r):
        return jnp.concatenate([hot(where_[w,pl.ds(r+i,1),:],jnp.broadcast_to(weigh[w,pl.ds(r+i,1),:],(16,LANES)).astype(jnp.bfloat16)) for i in range(2)],axis=1)
    def left(w,r,base):
        return jnp.concatenate([hot(place[w,pl.ds(r+i,1),:]-base,one) for i in range(2)],axis=1)
    for w in range(windows):
        for p in range(PARTS):
            lo,hi=bounds[w]
            if p==0:
                begin=jnp.int32(0); trips=(hi+step-1)//step
            else:
                begin=(lo//step)*step; trips=(height-begin)//step
            for m in range(2):
                pltpu.matmul_push_rhs(right(w,begin+2*m),staging_register=0,mxu_index=m,transpose=True)
            def body(i,c):
                base_r=begin+i*step
                for u in range(UNROLL):
                    m=u%2; s=(u//2)%2
                    r=base_r+2*u
                    nxt=r+4
                    if u>=UNROLL-2: nxt=jnp.minimum(nxt,height-2)
                    pltpu.matmul_push_rhs(right(w,nxt),staging_register=1-s,mxu_index=m,transpose=True)
                    pltpu.matmul_acc_lhs(accs[m],left(w,r,256.0*p),load_staged_rhs=s)
                return c
            lax.fori_loop(0,trips,body,0)
            for m in range(2):
                pltpu.matmul_acc_lhs(accs[m],jnp.zeros((256,256),jnp.bfloat16),load_staged_rhs=0)
            got=pltpu.matmul_pop(accs[0])+pltpu.matmul_pop(accs[1])
            for j in range(4):
                for c in range(2):
                    at=slice(64*p+32*c,64*p+32*c+32)
                    piece=got[64*j+32*c:64*j+32*c+32]
                    if w: piece=decay[w,2*p+c]*out[w-1,at,256*j:256*j+256]+piece
                    out[w,at,256*j:256*j+256]=piece
def view(x):
    windows,count=x.shape
    return x.reshape(windows,count//LANES,LANES).transpose(1,0,2).reshape(windows*count//LANES,LANES)
def binned(r,c,k,w,d):
    windows,count=r.shape
    height=count//LANES
    tall=windows*height
    return pl.pallas_call(
        kernel,
        out_shape=(
            jax.ShapeDtypeStruct((windows, SLOTS, COLS), jnp.float32),
            jax.ShapeDtypeStruct((windows, SUB, LANES), jnp.float32),
        ),
        in_specs=[pl.BlockSpec(memory_space=pltpu.HBM)] * 5,
        out_specs=[pl.BlockSpec(memory_space=pltpu.VMEM)] * 2,
        scratch_shapes=[pltpu.VMEM((tall, LANES), jnp.int32)] * 3
        + [pltpu.VMEM((tall, LANES), jnp.bfloat16), pltpu.SMEM(d.shape, jnp.float32)]
        + [pltpu.VMEM((tall, LANES), jnp.int32)]
        + [pltpu.VMEM((windows, height, LANES), jnp.float32)] * 3
        + [pltpu.SemaphoreType.DMA((5,))],
        compiler_params=pltpu.CompilerParams(vmem_limit_bytes=16 * 2**20),
    )(*(pltpu.with_memory_space_constraint(x, pltpu.HBM) for x in (*map(view, (r, c, k, w)), d)))


MESH = pl.DeviceIdType.MESH
CHUNK = 512


def across(tile):
    return jnp.concatenate([tile] * (CHUNK // LANES), axis=1)


def scan_kernel(
    n, size, running_hbm, fact_ref, out_ref,
    own, other, stage, inbox, total, earlier, carried, spread, back, prefix, handed, received,
    load_sem, swap_send, swap_recv, go_send, go_recv, up_send, up_recv, back_send, back_recv, hand_send, hand_recv,
):
    windows = running_hbm.shape[0]
    groups, chips = n // size, size // 2
    half = SLOTS // 2
    piece = half // chips
    chunks = COLS // CHUNK
    me = lax.axis_index("win")
    group, member = lax.div(me, size), lax.rem(me, size)
    chip, side = lax.div(member, 2), lax.rem(member, 2)
    partner = me + 1 - 2 * side
    mate = lambda k: group * size + 2 * lax.rem(chip + k, chips) + side
    counter = lambda k: lax.rem(me + k * size, n)

    barrier = pltpu.get_barrier_semaphore()
    peers = [partner] + [mate(k) for k in range(1, chips)] + [counter(k) for k in range(1, groups)]
    for peer in peers:
        pl.semaphore_signal(barrier, inc=1, device_id=(peer,), device_id_type=MESH)
    for c in range(chunks):
        own[c, :, :CHUNK] = running_hbm[windows - 1, :, c * CHUNK : (c + 1) * CHUNK]
    for channel in range(IMAGE_LAYERS):
        factor = fact_ref[windows - 1, channel : channel + 1, :]
        own[0, channel * ROWS : (channel + 1) * ROWS, CHUNK:] = jnp.broadcast_to(factor, (ROWS, LANES))

    def sent(ref, chunk):
        return ref if chunk == 0 else ref.at[:, pl.ds(0, CHUNK)]

    def remote(src, dst, send, recv, device):
        return pltpu.make_async_remote_copy(
            src_ref=src, dst_ref=dst, send_sem=send, recv_sem=recv, device_id=(device,), device_id_type=MESH
        )

    def swap_sides(chunk):
        away = own.at[chunk, pl.ds(pl.multiple_of((1 - side) * half, half), half)]
        return remote(
            sent(away, chunk), sent(other.at[chunk], chunk), swap_send.at[chunk], swap_recv.at[chunk], partner
        )

    def go(chunk, k, sender):
        peer = lax.rem(chip + k, chips)
        slot = chip if sender else peer
        return remote(
            sent(stage.at[chunk, peer], chunk), sent(inbox.at[chunk, slot], chunk),
            go_send.at[chunk, k], go_recv.at[chunk, slot], mate(k),
        )

    def up(chunk, k, slot):
        return remote(
            sent(total.at[chunk], chunk), sent(earlier.at[chunk, slot], chunk),
            up_send.at[chunk, k], up_recv.at[chunk, slot], counter(k),
        )

    def give(chunk, k, sender):
        peer = lax.rem(chip + k, chips)
        slot = chip if sender else peer
        return remote(
            back.at[chunk, peer], prefix.at[chunk, slot], back_send.at[chunk, k], back_recv.at[chunk, slot], mate(k)
        )

    def hand(chunk):
        return remote(
            handed.at[chunk], received.at[chunk], hand_send.at[chunk], hand_recv.at[chunk], partner
        )

    first = side == 0
    mine_at = pl.ds(pl.multiple_of(side * half, half), half)

    def combine(chunk):
        swap_sides(chunk).wait_recv()
        a, b = own[chunk, mine_at, :CHUNK], other[chunk, :, :CHUNK]
        fa, fb = own[0, mine_at, CHUNK:], other[0, :, CHUNK:]
        late = across(jnp.where(first, fb, fa))
        both = late * jnp.where(first, a, b) + jnp.where(first, b, a)
        for p in range(chips):
            stage[chunk, p, :, :CHUNK] = both[p * piece : (p + 1) * piece]
            if chunk == 0:
                stage[chunk, p, :, CHUNK:] = (fa * fb)[p * piece : (p + 1) * piece]
        for k in range(1, chips):
            go(chunk, k, True).start()
        wide = CHUNK if chunk else CHUNK + LANES
        inbox[chunk, chip, :, :wide] = stage[chunk, chip, :, :wide]

    def give_all(chunk):
        for k in range(1, chips):
            give(chunk, k, True).start()
        prefix[chunk, chip] = back[chunk, chip]

    def scan_group(chunk):
        for k in range(1, chips):
            go(chunk, k, False).wait_recv()
        running = jnp.zeros((piece, CHUNK), jnp.float32)
        factor = jnp.ones((piece, LANES), jnp.float32)
        for m in range(chips):
            back[chunk, m] = running
            by = inbox[0, m, :, CHUNK:]
            if chunk == 0:
                spread[m] = factor
            running = across(by) * running + inbox[chunk, m, :, :CHUNK]
            if chunk == 0:
                factor = factor * by
        total[chunk, :, :CHUNK] = running
        if chunk == 0:
            total[chunk, :, CHUNK:] = factor
        for k in range(1, groups):

            @pl.when(group + k < groups)
            def _():
                up(chunk, k, group).start()

        @pl.when(group == 0)
        def _():
            give_all(chunk)

    def finish_groups(chunk):
        if groups == 1:
            return
        carried[...] = jnp.zeros((piece, CHUNK), jnp.float32)
        for g in range(groups - 1):

            @pl.when(g < group)
            def _():
                up(chunk, 1, g).wait_recv()
                by = earlier[0, g, :, CHUNK:]
                carried[...] = across(by) * carried[...] + earlier[chunk, g, :, :CHUNK]

        @pl.when(group > 0)
        def _():
            before = carried[...]
            for m in range(chips):
                back[chunk, m] += across(spread[m]) * before
            give_all(chunk)

    def pass_on(chunk):
        for k in range(1, chips):
            give(chunk, k, False).wait_recv()
        before = prefix[chunk].reshape(half, CHUNK)
        a, b = own[chunk, mine_at, :CHUNK], other[chunk, :, :CHUNK]
        fa, fb = own[0, mine_at, CHUNK:], other[0, :, CHUNK:]
        after = across(jnp.where(first, fa, fb)) * before + jnp.where(first, a, b)
        handed[chunk] = jnp.where(first, after, before)
        hand(chunk).start()
        out_ref[mine_at, chunk * CHUNK : (chunk + 1) * CHUNK] = jnp.where(first, before, after)

    def take(chunk):
        hand(chunk).wait_recv()
        at = pl.ds(pl.multiple_of((1 - side) * half, half), half)
        out_ref[at, chunk * CHUNK : (chunk + 1) * CHUNK] = received[chunk]

    for chunk in range(chunks):
        if chunk == 0:
            pl.semaphore_wait(barrier, len(peers))
        swap_sides(chunk).start()
    for chunk in range(chunks):
        combine(chunk)
    for chunk in range(chunks):
        scan_group(chunk)
    for chunk in range(chunks):
        finish_groups(chunk)
    for chunk in range(chunks):
        pass_on(chunk)
    for chunk in range(chunks):
        take(chunk)

    for chunk in range(chunks):
        swap_sides(chunk).wait_send()
        hand(chunk).wait_send()
        for k in range(1, chips):
            go(chunk, k, True).wait_send()
            give(chunk, k, True).wait_send()
        for k in range(1, groups):

            @pl.when(group + k < groups)
            def _():
                up(chunk, k, group).wait_send()


def before_own(n, running, fact):
    size = max(s for s in range(2, 2 * SLOTS // (2 * SUB) + 1, 2) if n % s == 0 and SLOTS % (s * SUB) == 0)
    groups, chips = n // size, size // 2
    half = SLOTS // 2
    piece, chunks = half // chips, COLS // CHUNK
    wide = CHUNK + LANES
    dma = pltpu.SemaphoreType.DMA
    f32 = lambda *shape: pltpu.VMEM(shape, jnp.float32)
    return pl.pallas_call(
        functools.partial(scan_kernel, n, size),
        out_shape=jax.ShapeDtypeStruct((SLOTS, COLS), jnp.float32),
        in_specs=[pl.BlockSpec(memory_space=pltpu.VMEM)] * 2,
        out_specs=pl.BlockSpec(memory_space=pltpu.VMEM),
        scratch_shapes=[
            f32(chunks, SLOTS, wide), f32(chunks, half, wide), f32(chunks, chips, piece, wide),
            f32(chunks, chips, piece, wide), f32(chunks, piece, wide), f32(chunks, groups, piece, wide),
            f32(piece, CHUNK), f32(chips, piece, LANES), f32(chunks, chips, piece, CHUNK),
            f32(chunks, chips, piece, CHUNK), f32(chunks, half, CHUNK), f32(chunks, half, CHUNK),
            dma((chunks,)), dma((chunks,)), dma((chunks,)), dma((chunks, chips)), dma((chunks, chips)),
            dma((chunks, groups)), dma((chunks, groups)), dma((chunks, chips)), dma((chunks, chips)),
            dma((chunks,)), dma((chunks,)),
        ],
        compiler_params=pltpu.CompilerParams(collective_id=0, has_side_effects=True, vmem_limit_bytes=16 * 2**20),
    )(running, fact)


def heat_kernel(running_ref, before_ref, fact_ref, out_hbm, out_ref, sem):
    windows = running_ref.shape[0]
    stores = []
    for channel in range(IMAGE_LAYERS):
        at = slice(channel * ROWS, (channel + 1) * ROWS)
        for window in range(windows):
            factor = jnp.concatenate([fact_ref[window, channel : channel + 1, :]] * (COLS // LANES), axis=1)
            out_ref[window, at] = factor * before_ref[at] + running_ref[window, at]
            stores.append(
                pltpu.make_async_copy(out_ref.at[window, at], out_hbm.at[window, at], sem.at[window, channel])
            )
            stores[-1].start()
    for store in stores:
        store.wait()


def heat(running, before, fact):
    windows = running.shape[0]
    return pl.pallas_call(
        heat_kernel,
        out_shape=jax.ShapeDtypeStruct(running.shape, jnp.float32),
        in_specs=[pl.BlockSpec(memory_space=pltpu.VMEM)] * 3,
        out_specs=pl.BlockSpec(memory_space=pltpu.HBM),
        scratch_shapes=[pltpu.VMEM(running.shape, jnp.float32), pltpu.SemaphoreType.DMA((windows, IMAGE_LAYERS))],
        compiler_params=pltpu.CompilerParams(vmem_limit_bytes=8 * 2**20),
    )(running, before, fact)


def local(n, point_rows, point_cols, point_chans, point_weights, decay):
    running, fact = binned(point_rows, point_cols, point_chans, point_weights, decay)
    before = before_own(n, running, fact)
    return heat(running, before, fact).reshape(-1, IMAGE_LAYERS, ROWS, COLS)


def solution(mesh):
    placed = (P("win", None),) * 5
    return jax.shard_map(
        functools.partial(local, mesh.shape["win"]),
        mesh=mesh, in_specs=placed, out_specs=P("win", None, None, None), check_vma=False,
    )
```

time: 39.2 us -> 36.2 us (0.923)
  local copies, waits for them, and re-layouts: 2.31 us -> 0 us
  Pallas kernels: 36.7 us -> 36 us
    unnamed x1 -> x0, local copies, waits for them, and re-layouts: 2.31 us -> none
    pallas_call x1 -> x3, Pallas kernels: 36.7 us -> 36 us  [the longest x1 19.1 us: before_own(): pl.pallas_call(functools.partial(scan_kernel, n, size), out_shape=jax.Sha...]
where the time goes in v1:
time: 36.2 us; the launch traced here: 36 us
  Pallas kernels  36 us (99%)
    pallas_call x1, Pallas kernels, before_own(): pl.pallas_call(functools.partial(scan_kernel, n, size), out_shape=jax.Sha...  19.1 us
    pallas_call x1, Pallas kernels, binned(): pl.pallas_call(kernel, out_shape=(jax.ShapeDtypeStruct((windows, SLOTS, C...  15.9 us
    pallas_call x1, Pallas kernels, heat(): pl.pallas_call(heat_kernel, out_shape=jax.ShapeDtypeStruct(running.shape,...  1.05 us

profile of v1, /device:TPU:17, one launch (start us, length us, event | category | flops | bytes accessed | tf_op | source)
XLA Modules:
  0.0 36.0 jit_solution(12126036367908735516)
XLA Ops:
  0.0 15.9 %shard_map.55 = (f32[2,128,1024]{2,1,0:T(8,128)S(1)}, f32[2,8,128]{2,1,0:T(8,128)S(1)}) custom-call(s32[512,128]{1,0:T(8,128)} %bitcast.21, s32[512,128]{1,0:T(8,128)} %bitcast.22, s32[512,128]{1,0:T(8,128)} %bitcast.23, bf16[512,128]{1,0:T(8,128)(2,1)} %bitcast.24, f32[2,4]{1,0:T(2,128)} %decay_hbm.1), custom_call_target="tpu_custom_call" | custom-call | tf_op jit(solution)/shard_map/pallas_call | solution.py:134
  15.9 19.1 %shard_map.56.before_ref = f32[128,1024]{1,0:T(8,128)S(1)} custom-call(f32[2,128,1024]{2,1,0:T(8,128)S(1)} %get-tuple-element.7.running_hbm.running_ref, f32[2,8,128]{2,1,0:T(8,128)S(1)} %get-tuple-element.8.fact_ref), custom_call_target="tpu_custom_call" | custom-call | tf_op jit(solution)/shard_map/pallas_call | solution.py:346
  35.0 1.0 %shard_map.57 = f32[2,128,1024]{2,1,0:T(8,128)} custom-call(f32[2,128,1024]{2,1,0:T(8,128)S(1)} %get-tuple-element.7.running_hbm.running_ref, f32[128,1024]{1,0:T(8,128)S(1)} %shard_map.56.before_ref, f32[2,8,128]{2,1,0:T(8,128)S(1)} %get-tuple-element.8.fact_ref), custom_call_target="tpu_custom_call" | custom-call | tf_op jit(solution)/shard_map/pallas_call | solution.py:382

commit v2 on v1

--- a/solution.py
+++ b/solution.py
@@ -8,6 +8,9 @@
 SLOTS=128; ROWS=32; COLS=1024; PART=256; LANES=128; SUB=8
 PARTS=2
 UNROLL=8
+STEP=2*UNROLL
+PAD=STEP
+MIDDLE=64
 def hot(index, on):
     spread = jnp.broadcast_to(index, (16, LANES)).astype(jnp.bfloat16)
     slots = lax.broadcasted_iota(jnp.int32, (16, LANES), 0).astype(jnp.float32).astype(jnp.bfloat16)
@@ -52,14 +55,14 @@
         width*=2
     return xs
 
-def kernel(rows_hbm, cols_hbm, chans_hbm, weights_hbm, decay_hbm, out, fact, rows, cols, chans, weights, decay, keys, place, where_, weigh, sem):
+def kernel(rows_hbm, cols_hbm, chans_hbm, weights_hbm, decay_hbm, out, fact, rows, cols, chans, weights, decay, keys, place, where_, weigh, ahead, sem):
     copies=[pltpu.make_async_copy(a,b,sem.at[i]) for i,(a,b) in enumerate(((decay_hbm,decay),(weights_hbm,weights),(cols_hbm,cols),(chans_hbm,chans),(rows_hbm,rows)))]
     for copy in copies: copy.start()
     for copy in copies: copy.wait()
-    pl.run_scoped(functools.partial(bin_points,rows,cols,chans,weights,decay,out,fact,keys,place,where_,weigh),
-        pltpu.ACC(0)((256,256),jnp.float32),pltpu.ACC(1)((256,256),jnp.float32))
-
-def bin_points(rows, cols, chans, weights, decay, out, fact, keys, place, where_, weigh, *accs):
+    pl.run_scoped(functools.partial(bin_points,rows,cols,chans,weights,decay,out,fact,keys,place,where_,weigh,ahead),
+        *[pltpu.ACC(m)((256,256),jnp.float32) for _ in range(3) for m in range(2)])
+
+def bin_points(rows, cols, chans, weights, decay, out, fact, keys, place, where_, weigh, ahead, *accs):
     windows = out.shape[0]
     for channel in range(IMAGE_LAYERS):
         factor = jnp.float32(1.0)
@@ -74,56 +77,86 @@
         w=(weights[at,:].astype(jnp.float32)*512.0).astype(jnp.int32)
         lidx=((k>>1)<<8)|((c>>8)<<6)|((k&1)<<5)|rows[at,:]
         keys[at,:]=(lidx<<20)|((c&255)<<12)|w
+    span=place.shape[0]//windows
     bounds=[]
     n=height//SUB
     for w in range(windows):
         xs=[keys[pl.ds(w+windows*SUB*v,SUB,stride=windows),:] for v in range(n)]
         xs=sort_rows(xs)
-        first=jnp.zeros((SUB,LANES),jnp.int32)
+        counts=[jnp.zeros((SUB,LANES),jnp.int32) for _ in range(3)]
         for v in range(n):
             x=xs[v]
-            first=first+jnp.where(x<(1<<28),1,0)
-            at=pl.ds(v,SUB,stride=n)
-            place[w,at,:]=(x>>20).astype(jnp.float32)
-            where_[w,at,:]=((x>>12)&255).astype(jnp.float32)
-            weigh[w,at,:]=(x&4095).astype(jnp.float32)*(1.0/512.0)
-        first=jnp.sum(first,axis=0,keepdims=True)
-        bounds.append((jnp.min(first),jnp.max(first)))
+            for q in range(3):
+                counts[q]=counts[q]+jnp.where(x<((q+1)<<27),1,0)
+            at=pl.ds(w*span+PAD+v,SUB,stride=n)
+            place[at,:]=(x>>20).astype(jnp.float32)
+            where_[at,:]=((x>>12)&255).astype(jnp.float32)
+            weigh[at,:]=(x&4095).astype(jnp.float32)*(1.0/512.0)
+        for at in (slice(w*span,w*span+PAD),slice(w*span+PAD+height,(w+1)*span)):
+            rest=(at.stop-at.start,LANES)
+            place[at,:]=jnp.full(rest,-1000.0,jnp.float32)
+            where_[at,:]=jnp.zeros(rest,jnp.float32)
+            weigh[at,:]=jnp.zeros(rest,jnp.float32)
+        low,mid,high=(jnp.sum(count,axis=0,keepdims=True) for count in counts)
+        bounds.append((jnp.max(jnp.maximum(low,mid-MIDDLE)),jnp.min(jnp.minimum(mid,high-MIDDLE)),jnp.min(mid),jnp.max(mid)))
     one=jnp.ones((16,LANES),jnp.bfloat16)
-    step=2*UNROLL
-    def right(w,r):
-        return jnp.concatenate([hot(where_[w,pl.ds(r+i,1),:],jnp.broadcast_to(weigh[w,pl.ds(r+i,1),:],(16,LANES)).astype(jnp.bfloat16)) for i in range(2)],axis=1)
-    def left(w,r,base):
-        return jnp.concatenate([hot(place[w,pl.ds(r+i,1),:]-base,one) for i in range(2)],axis=1)
+    def right(r):
+        return jnp.concatenate([hot(where_[pl.ds(r+i,1),:],jnp.broadcast_to(weigh[pl.ds(r+i,1),:],(16,LANES)).astype(jnp.bfloat16)) for i in range(2)],axis=1)
+    def left(r,base):
+        return jnp.concatenate([hot(place[pl.ds(r+i,1),:]-base,one) for i in range(2)],axis=1)
+    def prepare(m,staging,r,base):
+        pltpu.matmul_push_rhs(right(r),staging_register=staging,mxu_index=m,transpose=True)
+        ahead[m]=left(r,base)
+    def multiply(targets,begin,trips,base,then):
+        def body(i,c):
+            base_r=begin+i*STEP
+            for u in range(UNROLL):
+                m=u%2; s=(u//2)%2
+                r=base_r+2*u
+                nxt=r+4
+                if u>=UNROLL-2: nxt=jnp.where(i==trips-1,then[0]+2*m,nxt)
+                pltpu.matmul_push_rhs(right(nxt),staging_register=1-s,mxu_index=m,transpose=True)
+                pltpu.matmul_acc_lhs(targets[m],ahead[m] if u<2 else left(r,base),load_staged_rhs=s)
+                if u>=UNROLL-2: ahead[m]=left(nxt,jnp.where(i==trips-1,then[1],base))
+            return c
+        lax.fori_loop(0,trips,body,0)
+    def put(w,got,quarter,blend):
+        for block in range(8):
+            index=4*quarter+block
+            part,j,c=index//8,index//2%4,index%2
+            at=slice(64*part+32*c,64*part+32*c+32)
+            piece=got[32*block:32*block+32]
+            out[w,at,256*j:256*j+256]=blend(out,w,at,j,2*part+c,piece)
+    def begin_sum(out,w,at,j,channel,piece):
+        return decay[w,channel]*out[w-1,at,256*j:256*j+256]+piece if w else piece
+    def add(out,w,at,j,channel,piece):
+        return out[w,at,256*j:256*j+256]+piece
+    phases=[]
     for w in range(windows):
-        for p in range(PARTS):
-            lo,hi=bounds[w]
-            if p==0:
-                begin=jnp.int32(0); trips=(hi+step-1)//step
-            else:
-                begin=(lo//step)*step; trips=(height-begin)//step
-            for m in range(2):
-                pltpu.matmul_push_rhs(right(w,begin+2*m),staging_register=0,mxu_index=m,transpose=True)
-            def body(i,c):
-                base_r=begin+i*step
-                for u in range(UNROLL):
-                    m=u%2; s=(u//2)%2
-                    r=base_r+2*u
-                    nxt=r+4
-                    if u>=UNROLL-2: nxt=jnp.minimum(nxt,height-2)
-                    pltpu.matmul_push_rhs(right(w,nxt),staging_register=1-s,mxu_index=m,transpose=True)
-                    pltpu.matmul_acc_lhs(accs[m],left(w,r,256.0*p),load_staged_rhs=s)
-                return c
-            lax.fori_loop(0,trips,body,0)
-            for m in range(2):
-                pltpu.matmul_acc_lhs(accs[m],jnp.zeros((256,256),jnp.bfloat16),load_staged_rhs=0)
-            got=pltpu.matmul_pop(accs[0])+pltpu.matmul_pop(accs[1])
-            for j in range(4):
-                for c in range(2):
-                    at=slice(64*p+32*c,64*p+32*c+32)
-                    piece=got[64*j+32*c:64*j+32*c+32]
-                    if w: piece=decay[w,2*p+c]*out[w-1,at,256*j:256*j+256]+piece
-                    out[w,at,256*j:256*j+256]=piece
+        least,most,lo,hi=bounds[w]
+        split=least<=most
+        a=jnp.clip(jnp.int32((height-MIDDLE)//2),least,most)
+        up=lambda x: (x+STEP-1)//STEP
+        trips=jnp.where(split,up(a),up(hi))
+        phases.append((jnp.where(split,a-trips*STEP,0)+w*span+PAD,trips))
+        phases.append((a+w*span+PAD,jnp.where(split,MIDDLE//STEP,0)))
+        begin=jnp.where(split,a+MIDDLE,(lo//STEP)*STEP)
+        phases.append((begin+w*span+PAD,up(height-begin)))
+    starts=[(jnp.int32(0),jnp.float32(0.0))]
+    for k in reversed(range(len(phases))):
+        begin,trips=phases[k]
+        some=trips>0
+        starts.insert(0,(jnp.where(some,begin,starts[0][0]),jnp.where(some,jnp.float32(128.0*(k%3)),starts[0][1])))
+    for m in range(2): prepare(m,0,starts[0][0]+2*m,starts[0][1])
+    for w in range(windows):
+        for p in range(3):
+            begin,trips=phases[3*w+p]
+            multiply(accs[2*p:2*p+2],begin,trips,jnp.float32(128.0*p),starts[3*w+p+1])
+        for p,quarter in ((0,0),(2,2),(1,1)):
+            put(w,pltpu.matmul_pop(accs[2*p])+pltpu.matmul_pop(accs[2*p+1]),quarter,add if p==1 else begin_sum)
+    for m in range(2):
+        pltpu.matmul_acc_lhs(accs[m],jnp.zeros((256,256),jnp.bfloat16),load_staged_rhs=0)
+    out[0,:1,:256]=out[0,:1,:256]+(pltpu.matmul_pop(accs[0])+pltpu.matmul_pop(accs[1]))[:1]
 def view(x):
     windows,count=x.shape
     return x.reshape(windows,count//LANES,LANES).transpose(1,0,2).reshape(windows*count//LANES,LANES)
@@ -142,7 +175,8 @@
         scratch_shapes=[pltpu.VMEM((tall, LANES), jnp.int32)] * 3
         + [pltpu.VMEM((tall, LANES), jnp.bfloat16), pltpu.SMEM(d.shape, jnp.float32)]
         + [pltpu.VMEM((tall, LANES), jnp.int32)]
-        + [pltpu.VMEM((windows, height, LANES), jnp.float32)] * 3
+        + [pltpu.VMEM((windows * (PAD + height + PAD + SUB), LANES), jnp.float32)] * 3
+        + [pltpu.VMEM((2, 256, 256), jnp.bfloat16)]
         + [pltpu.SemaphoreType.DMA((5,))],
         compiler_params=pltpu.CompilerParams(vmem_limit_bytes=16 * 2**20),
     )(*(pltpu.with_memory_space_constraint(x, pltpu.HBM) for x in (*map(view, (r, c, k, w)), d)))

time: 36.2 us -> 33.5 us (0.925)
  Pallas kernels: 36 us -> 33.2 us
    pallas_call x1, Pallas kernels: 15.9 us -> 13.6 us  [binned(): pl.pallas_call(kernel, out_shape=(jax.ShapeDtypeStruct((windows, SLOTS, C...]
    pallas_call x1, Pallas kernels: 19.1 us -> 18.5 us  [before_own(): pl.pallas_call(functools.partial(scan_kernel, n, size), out_shape=jax.Sha...]
where the time goes in v2:
time: 33.5 us; the launch traced here: 33.2 us
  Pallas kernels  33.2 us (99%)
    pallas_call x1, Pallas kernels, before_own(): pl.pallas_call(functools.partial(scan_kernel, n, size), out_shape=jax.Sha...  18.5 us
    pallas_call x1, Pallas kernels, binned(): pl.pallas_call(kernel, out_shape=(jax.ShapeDtypeStruct((windows, SLOTS, C...  13.6 us
    pallas_call x1, Pallas kernels, heat(): pl.pallas_call(heat_kernel, out_shape=jax.ShapeDtypeStruct(running.shape,...  1.05 us

profile of v2, /device:TPU:17, one launch (start us, length us, event | category | flops | bytes accessed | tf_op | source)
XLA Modules:
  0.0 33.2 jit_solution(219778583915825542)
XLA Ops:
  0.0 13.6 %shard_map.55 = (f32[2,128,1024]{2,1,0:T(8,128)S(1)}, f32[2,8,128]{2,1,0:T(8,128)S(1)}) custom-call(s32[512,128]{1,0:T(8,128)} %bitcast.21, s32[512,128]{1,0:T(8,128)} %bitcast.22, s32[512,128]{1,0:T(8,128)} %bitcast.23, bf16[512,128]{1,0:T(8,128)(2,1)} %bitcast.24, f32[2,4]{1,0:T(2,128)} %decay_hbm.1), custom_call_target="tpu_custom_call" | custom-call | tf_op jit(solution)/shard_map/pallas_call | solution.py:167
  13.7 18.5 %shard_map.56.before_ref = f32[128,1024]{1,0:T(8,128)S(1)} custom-call(f32[2,128,1024]{2,1,0:T(8,128)S(1)} %get-tuple-element.7.running_hbm.running_ref, f32[2,8,128]{2,1,0:T(8,128)S(1)} %get-tuple-element.8.fact_ref), custom_call_target="tpu_custom_call" | custom-call | tf_op jit(solution)/shard_map/pallas_call | solution.py:380
  32.2 1.0 %shard_map.57 = f32[2,128,1024]{2,1,0:T(8,128)} custom-call(f32[2,128,1024]{2,1,0:T(8,128)S(1)} %get-tuple-element.7.running_hbm.running_ref, f32[128,1024]{1,0:T(8,128)S(1)} %shard_map.56.before_ref, f32[2,8,128]{2,1,0:T(8,128)S(1)} %get-tuple-element.8.fact_ref), custom_call_target="tpu_custom_call" | custom-call | tf_op jit(solution)/shard_map/pallas_call | solution.py:416

commit v3 on v1

--- a/solution.py
+++ b/solution.py
@@ -8,6 +8,7 @@
 SLOTS=128; ROWS=32; COLS=1024; PART=256; LANES=128; SUB=8
 PARTS=2
 UNROLL=8
+STEP=2*UNROLL
 def hot(index, on):
     spread = jnp.broadcast_to(index, (16, LANES)).astype(jnp.bfloat16)
     slots = lax.broadcasted_iota(jnp.int32, (16, LANES), 0).astype(jnp.float32).astype(jnp.bfloat16)
@@ -52,78 +53,100 @@
         width*=2
     return xs
 
-def kernel(rows_hbm, cols_hbm, chans_hbm, weights_hbm, decay_hbm, out, fact, rows, cols, chans, weights, decay, keys, place, where_, weigh, sem):
+def splits(height):
+    first, second = (height * cut // 8 // STEP * STEP for cut in (3, 5))
+    return (0, first, second, height)
+
+
+def right(where_, weigh, r):
+    return jnp.concatenate([hot(where_[pl.ds(r+i,1),:],jnp.broadcast_to(weigh[pl.ds(r+i,1),:],(16,LANES)).astype(jnp.bfloat16)) for i in range(2)],axis=1)
+
+
+def left(place, r, base):
+    one=jnp.ones((16,LANES),jnp.bfloat16)
+    return jnp.concatenate([hot(place[pl.ds(r+i,1),:]-base,one) for i in range(2)],axis=1)
+
+
+def blocks(got, quarter):
+    for block in range(8):
+        index=4*quarter+block
+        part,j,c=index//8,index//2%4,index%2
+        yield slice(64*part+32*c,64*part+32*c+32),slice(256*j,256*j+256),2*part+c,got[32*block:32*block+32]
+
+
+def kernel(rows_hbm, cols_hbm, chans_hbm, weights_hbm, decay_hbm, place, where_, weigh, spare, fact, rows, cols, chans, weights, decay, keys, odd, sem):
     copies=[pltpu.make_async_copy(a,b,sem.at[i]) for i,(a,b) in enumerate(((decay_hbm,decay),(weights_hbm,weights),(cols_hbm,cols),(chans_hbm,chans),(rows_hbm,rows)))]
     for copy in copies: copy.start()
+    windows = spare.shape[0]
+    spare[...] = jnp.zeros(spare.shape, jnp.float32)
     for copy in copies: copy.wait()
-    pl.run_scoped(functools.partial(bin_points,rows,cols,chans,weights,decay,out,fact,keys,place,where_,weigh),
-        pltpu.ACC(0)((256,256),jnp.float32),pltpu.ACC(1)((256,256),jnp.float32))
-
-def bin_points(rows, cols, chans, weights, decay, out, fact, keys, place, where_, weigh, *accs):
-    windows = out.shape[0]
+    pl.run_scoped(functools.partial(sort_points,rows,cols,chans,weights,decay,place,where_,weigh,spare,fact,keys,odd),
+        *[pltpu.ACC(m)((256,256),jnp.float32) for m in range(2)])
+
+
+def sort_points(rows, cols, chans, weights, decay, place, where_, weigh, spare, fact, keys, odd, *accs):
+    windows = spare.shape[0]
     for channel in range(IMAGE_LAYERS):
         factor = jnp.float32(1.0)
         for w in range(windows):
             factor = factor * decay[w, channel]
             fact[w, channel : channel + 1, :] = jnp.full((1, LANES), factor, jnp.float32)
+            at = IMAGE_LAYERS + channel
+            fact[w, at : at + 1, :] = jnp.full((1, LANES), decay[w, channel], jnp.float32)
     total = rows.shape[0]; height = total//windows
-    for a in accs: out[0,:,0:256]=pltpu.matmul_pop(a)[:128]
+    _, first, second, _ = splits(height)
     for v in range(total//16):
         at=pl.ds(16*v,16)
         c=cols[at,:]; k=chans[at,:]
         w=(weights[at,:].astype(jnp.float32)*512.0).astype(jnp.int32)
         lidx=((k>>1)<<8)|((c>>8)<<6)|((k&1)<<5)|rows[at,:]
         keys[at,:]=(lidx<<20)|((c&255)<<12)|w
+    n=height//SUB
+    ranks=lax.broadcasted_iota(jnp.int32,(SUB,LANES),0)*n
     bounds=[]
-    n=height//SUB
     for w in range(windows):
         xs=[keys[pl.ds(w+windows*SUB*v,SUB,stride=windows),:] for v in range(n)]
         xs=sort_rows(xs)
-        first=jnp.zeros((SUB,LANES),jnp.int32)
+        least=jnp.full((SUB,LANES),height,jnp.int32); most=jnp.full((SUB,LANES),-1,jnp.int32)
         for v in range(n):
             x=xs[v]
-            first=first+jnp.where(x<(1<<28),1,0)
-            at=pl.ds(v,SUB,stride=n)
-            place[w,at,:]=(x>>20).astype(jnp.float32)
-            where_[w,at,:]=((x>>12)&255).astype(jnp.float32)
-            weigh[w,at,:]=(x&4095).astype(jnp.float32)*(1.0/512.0)
-        first=jnp.sum(first,axis=0,keepdims=True)
-        bounds.append((jnp.min(first),jnp.max(first)))
-    one=jnp.ones((16,LANES),jnp.bfloat16)
-    step=2*UNROLL
-    def right(w,r):
-        return jnp.concatenate([hot(where_[w,pl.ds(r+i,1),:],jnp.broadcast_to(weigh[w,pl.ds(r+i,1),:],(16,LANES)).astype(jnp.bfloat16)) for i in range(2)],axis=1)
-    def left(w,r,base):
-        return jnp.concatenate([hot(place[w,pl.ds(r+i,1),:]-base,one) for i in range(2)],axis=1)
+            index=x>>20
+            rank=ranks+v
+            base=jnp.where(rank<first,0,jnp.where(rank<second,128,256))
+            out_of=(index<base)|(index>=base+256)
+            least=jnp.minimum(least,jnp.where(out_of,rank,height))
+            most=jnp.maximum(most,jnp.where(out_of,rank,-1))
+            at=pl.ds(w*height+v,SUB,stride=n)
+            index=index.astype(jnp.float32)
+            place[at,:]=index
+            odd[at,:]=jnp.where(out_of,index,-1000.0)
+            where_[at,:]=((x>>12)&255).astype(jnp.float32)
+            weigh[at,:]=(x&4095).astype(jnp.float32)*(1.0/512.0)
+        bounds.append((jnp.min(least),jnp.max(most)))
+    rest=slice(total,place.shape[0]); size=(place.shape[0]-total,LANES)
+    place[rest,:]=jnp.full(size,-1000.0,jnp.float32)
+    where_[rest,:]=jnp.zeros(size,jnp.float32)
+    weigh[rest,:]=jnp.zeros(size,jnp.float32)
     for w in range(windows):
-        for p in range(PARTS):
-            lo,hi=bounds[w]
-            if p==0:
-                begin=jnp.int32(0); trips=(hi+step-1)//step
-            else:
-                begin=(lo//step)*step; trips=(height-begin)//step
-            for m in range(2):
-                pltpu.matmul_push_rhs(right(w,begin+2*m),staging_register=0,mxu_index=m,transpose=True)
-            def body(i,c):
-                base_r=begin+i*step
-                for u in range(UNROLL):
-                    m=u%2; s=(u//2)%2
-                    r=base_r+2*u
-                    nxt=r+4
-                    if u>=UNROLL-2: nxt=jnp.minimum(nxt,height-2)
-                    pltpu.matmul_push_rhs(right(w,nxt),staging_register=1-s,mxu_index=m,transpose=True)
-                    pltpu.matmul_acc_lhs(accs[m],left(w,r,256.0*p),load_staged_rhs=s)
-                return c
-            lax.fori_loop(0,trips,body,0)
-            for m in range(2):
-                pltpu.matmul_acc_lhs(accs[m],jnp.zeros((256,256),jnp.bfloat16),load_staged_rhs=0)
-            got=pltpu.matmul_pop(accs[0])+pltpu.matmul_pop(accs[1])
-            for j in range(4):
-                for c in range(2):
-                    at=slice(64*p+32*c,64*p+32*c+32)
-                    piece=got[64*j+32*c:64*j+32*c+32]
-                    if w: piece=decay[w,2*p+c]*out[w-1,at,256*j:256*j+256]+piece
-                    out[w,at,256*j:256*j+256]=piece
+        least,most=bounds[w]
+
+        @pl.when(most>=least)
+        def _():
+            begin=(least>>2)<<2
+            for quarter in (0,2):
+                for m in range(2): pltpu.matmul_pop(accs[m])
+
+                def body(i,c):
+                    for m in range(2):
+                        r=w*height+begin+4*i+2*m
+                        pltpu.matmul_push_rhs(right(where_,weigh,r),staging_register=0,mxu_index=m,transpose=True)
+                        pltpu.matmul_acc_lhs(accs[m],left(odd,r,128.0*quarter),load_staged_rhs=0)
+                    return c
+                lax.fori_loop(0,(most-begin)//4+1,body,0)
+                for at,across_,_,piece in blocks(pltpu.matmul_pop(accs[0])+pltpu.matmul_pop(accs[1]),quarter):
+                    spare[w,at,across_]=piece
+
+
 def view(x):
     windows,count=x.shape
     return x.reshape(windows,count//LANES,LANES).transpose(1,0,2).reshape(windows*count//LANES,LANES)
@@ -131,18 +154,19 @@
     windows,count=r.shape
     height=count//LANES
     tall=windows*height
+    points=jax.ShapeDtypeStruct((tall+SUB,LANES),jnp.float32)
     return pl.pallas_call(
         kernel,
         out_shape=(
+            points, points, points,
             jax.ShapeDtypeStruct((windows, SLOTS, COLS), jnp.float32),
             jax.ShapeDtypeStruct((windows, SUB, LANES), jnp.float32),
         ),
         in_specs=[pl.BlockSpec(memory_space=pltpu.HBM)] * 5,
-        out_specs=[pl.BlockSpec(memory_space=pltpu.VMEM)] * 2,
+        out_specs=[pl.BlockSpec(memory_space=pltpu.VMEM)] * 5,
         scratch_shapes=[pltpu.VMEM((tall, LANES), jnp.int32)] * 3
         + [pltpu.VMEM((tall, LANES), jnp.bfloat16), pltpu.SMEM(d.shape, jnp.float32)]
-        + [pltpu.VMEM((tall, LANES), jnp.int32)]
-        + [pltpu.VMEM((windows, height, LANES), jnp.float32)] * 3
+        + [pltpu.VMEM((tall, LANES), jnp.int32), pltpu.VMEM((tall, LANES), jnp.float32)]
         + [pltpu.SemaphoreType.DMA((5,))],
         compiler_params=pltpu.CompilerParams(vmem_limit_bytes=16 * 2**20),
     )(*(pltpu.with_memory_space_constraint(x, pltpu.HBM) for x in (*map(view, (r, c, k, w)), d)))
@@ -156,9 +180,63 @@
     return jnp.concatenate([tile] * (CHUNK // LANES), axis=1)
 
 
+def bin_points(place, where_, weigh, spare, fact, running, ahead, *accs):
+    windows = running.shape[0]
+    height = (place.shape[0] - SUB) // windows
+    cuts = splits(height)
+    for acc in accs:
+        running[0, :, :PART] = pltpu.matmul_pop(acc)[:SLOTS]
+
+    def prepare(m, staging, r, base):
+        pltpu.matmul_push_rhs(right(where_, weigh, r), staging_register=staging, mxu_index=m, transpose=True)
+        ahead[m] = left(place, r, base)
+
+    def multiply(targets, begin, trips, base, then):
+        def body(i, carry):
+            for u in range(UNROLL):
+                m, s = u % 2, u // 2 % 2
+                r = begin + i * STEP + 2 * u
+                pltpu.matmul_push_rhs(
+                    right(where_, weigh, r + 4), staging_register=1 - s, mxu_index=m, transpose=True
+                )
+                pltpu.matmul_acc_lhs(targets[m], ahead[m] if u < 2 else left(place, r, base), load_staged_rhs=s)
+                if u >= UNROLL - 2:
+                    ahead[m] = left(place, r + 4, jnp.where(i == trips - 1, then, base))
+            return carry
+
+        lax.fori_loop(0, trips, body, 0)
+
+    def gather(w, phase, add):
+        got = pltpu.matmul_pop(accs[2 * phase]) + pltpu.matmul_pop(accs[2 * phase + 1])
+        for at, across_, channel, piece in blocks(got, phase):
+            if add:
+                running[w, at, across_] += piece
+                continue
+            piece = piece + spare[w, at, across_]
+            if w:
+                row = fact[w, IMAGE_LAYERS + channel : IMAGE_LAYERS + channel + 1, :]
+                piece = jnp.concatenate([row] * (PART // LANES), axis=1) * running[w - 1, at, across_] + piece
+            running[w, at, across_] = piece
+
+    for m in range(2):
+        prepare(m, 0, 2 * m, jnp.float32(0.0))
+    for w in range(windows):
+        for p in range(3):
+            trips = (cuts[p + 1] - cuts[p]) // STEP
+            multiply(
+                accs[2 * p : 2 * p + 2], w * height + cuts[p], trips,
+                jnp.float32(128.0 * p), jnp.float32(128.0 * ((p + 1) % 3)),
+            )
+        for p in (0, 2, 1):
+            gather(w, p, p == 1)
+    for m in range(2):
+        pltpu.matmul_acc_lhs(accs[m], jnp.zeros((256, 256), jnp.bfloat16), load_staged_rhs=0)
+    running[0, :1, :PART] += (pltpu.matmul_pop(accs[0]) + pltpu.matmul_pop(accs[1]))[:1]
+
+
 def scan_kernel(
-    n, size, running_hbm, fact_ref, out_ref,
-    own, other, stage, inbox, total, earlier, carried, spread, back, prefix, handed, received,
+    n, size, place, where_, weigh, spare, fact_ref, running_hbm, out_ref,
+    ahead, own, other, stage, inbox, total, earlier, carried, spread, back, prefix, handed, received,
     load_sem, swap_send, swap_recv, go_send, go_recv, up_send, up_recv, back_send, back_recv, hand_send, hand_recv,
 ):
     windows = running_hbm.shape[0]
@@ -177,6 +255,10 @@
     peers = [partner] + [mate(k) for k in range(1, chips)] + [counter(k) for k in range(1, groups)]
     for peer in peers:
         pl.semaphore_signal(barrier, inc=1, device_id=(peer,), device_id_type=MESH)
+    pl.run_scoped(
+        functools.partial(bin_points, place, where_, weigh, spare, fact_ref, running_hbm, ahead),
+        *[pltpu.ACC(m)((256, 256), jnp.float32) for _ in range(3) for m in range(2)],
+    )
     for c in range(chunks):
         own[c, :, :CHUNK] = running_hbm[windows - 1, :, c * CHUNK : (c + 1) * CHUNK]
     for channel in range(IMAGE_LAYERS):
@@ -335,7 +417,8 @@
                 up(chunk, k, group).wait_send()
 
 
-def before_own(n, running, fact):
+def before_own(n, place, where_, weigh, spare, fact):
+    windows = spare.shape[0]
     size = max(s for s in range(2, 2 * SLOTS // (2 * SUB) + 1, 2) if n % s == 0 and SLOTS % (s * SUB) == 0)
     groups, chips = n // size, size // 2
     half = SLOTS // 2
@@ -345,10 +428,14 @@
     f32 = lambda *shape: pltpu.VMEM(shape, jnp.float32)
     return pl.pallas_call(
         functools.partial(scan_kernel, n, size),
-        out_shape=jax.ShapeDtypeStruct((SLOTS, COLS), jnp.float32),
-        in_specs=[pl.BlockSpec(memory_space=pltpu.VMEM)] * 2,
-        out_specs=pl.BlockSpec(memory_space=pltpu.VMEM),
+        out_shape=(
+            jax.ShapeDtypeStruct((windows, SLOTS, COLS), jnp.float32),
+            jax.ShapeDtypeStruct((SLOTS, COLS), jnp.float32),
+        ),
+        in_specs=[pl.BlockSpec(memory_space=pltpu.VMEM)] * 5,
+        out_specs=[pl.BlockSpec(memory_space=pltpu.VMEM)] * 2,
         scratch_shapes=[
+            pltpu.VMEM((2, 256, 256), jnp.bfloat16),
             f32(chunks, SLOTS, wide), f32(chunks, half, wide), f32(chunks, chips, piece, wide),
             f32(chunks, chips, piece, wide), f32(chunks, piece, wide), f32(chunks, groups, piece, wide),
             f32(piece, CHUNK), f32(chips, piece, LANES), f32(chunks, chips, piece, CHUNK),
@@ -358,7 +445,7 @@
             dma((chunks,)), dma((chunks,)),
         ],
         compiler_params=pltpu.CompilerParams(collective_id=0, has_side_effects=True, vmem_limit_bytes=16 * 2**20),
-    )(running, fact)
+    )(place, where_, weigh, spare, fact)
 
 
 def heat_kernel(running_ref, before_ref, fact_ref, out_hbm, out_ref, sem):
@@ -390,8 +477,8 @@
 
 
 def local(n, point_rows, point_cols, point_chans, point_weights, decay):
-    running, fact = binned(point_rows, point_cols, point_chans, point_weights, decay)
-    before = before_own(n, running, fact)
+    *points, fact = binned(point_rows, point_cols, point_chans, point_weights, decay)
+    running, before = before_own(n, *points, fact)
     return heat(running, before, fact).reshape(-1, IMAGE_LAYERS, ROWS, COLS)
 
 

time: 36.2 us -> 31.2 us (0.86)
  Pallas kernels: 36 us -> 31.1 us
    pallas_call x2, Pallas kernels: 35 us -> 30 us  [the longest x1 26.9 us: before_own(): pl.pallas_call(functools.partial(scan_kernel, n, size), out_shape=(jax.Sh...]
where the time goes in v3:
time: 31.2 us; the launch traced here: 31.1 us
  Pallas kernels  31.1 us (100%)
    pallas_call x1, Pallas kernels, before_own(): pl.pallas_call(functools.partial(scan_kernel, n, size), out_shape=(jax.Sh...  26.9 us
    pallas_call x1, Pallas kernels, binned(): pl.pallas_call(kernel, out_shape=(points, points, points, jax.ShapeDtypeS...  3.16 us
    pallas_call x1, Pallas kernels, heat(): pl.pallas_call(heat_kernel, out_shape=jax.ShapeDtypeStruct(running.shape,...  1.04 us

profile of v3, /device:TPU:17, one launch (start us, length us, event | category | flops | bytes accessed | tf_op | source)
XLA Modules:
  0.0 31.1 jit_solution(13062397352893473927)
XLA Ops:
  0.0 3.2 %shard_map.55 = (f32[520,128]{1,0:T(8,128)S(1)}, f32[520,128]{1,0:T(8,128)S(1)}, f32[520,128]{1,0:T(8,128)S(1)}, f32[2,128,1024]{2,1,0:T(8,128)S(1)}, f32[2,8,128]{2,1,0:T(8,128)S(1)}) custom-call(s32[512,128]{1,0:T(8,128)} %bitcast.21, s32[512,128]{1,0:T(8,128)} %bitcast.22, s32[512,128]{1,0:T(8,128)} %bitcast.23, bf16[512,128]{1,0:T(8,128)(2,1)} %bitcast.24, ...), custom_call_target="tpu_custom_call" | custom-call | tf_op jit(solution)/shard_map/pallas_call | solution.py:158
  3.2 26.9 %shard_map.56 = (f32[2,128,1024]{2,1,0:T(8,128)S(1)}, f32[128,1024]{1,0:T(8,128)S(1)}) custom-call(f32[520,128]{1,0:T(8,128)S(1)} %get-tuple-element.12.place, f32[520,128]{1,0:T(8,128)S(1)} %get-tuple-element.13.where_, f32[520,128]{1,0:T(8,128)S(1)} %get-tuple-element.14.weigh, f32[2,128,1024]{2,1,0:T(8,128)S(1)} %get-tuple-element.15.spare, ...), custom_call_target="tpu_custom_call" | custom-call | tf_op jit(solution)/shard_map/pallas_call | solution.py:429
  30.0 1.0 %shard_map.57 = f32[2,128,1024]{2,1,0:T(8,128)} custom-call(f32[2,128,1024]{2,1,0:T(8,128)S(1)} %get-tuple-element.17.running_ref, f32[128,1024]{1,0:T(8,128)S(1)} %get-tuple-element.18.before_ref, f32[2,8,128]{2,1,0:T(8,128)S(1)} %get-tuple-element.16.fact_ref), custom_call_target="tpu_custom_call" | custom-call | tf_op jit(solution)/shard_map/pallas_call | solution.py:469

commit v4 on v3

--- a/solution.py
+++ b/solution.py
@@ -180,70 +180,112 @@
     return jnp.concatenate([tile] * (CHUNK // LANES), axis=1)
 
 
-def bin_points(place, where_, weigh, spare, fact, running, ahead, *accs):
-    windows = running.shape[0]
-    height = (place.shape[0] - SUB) // windows
-    cuts = splits(height)
-    for acc in accs:
-        running[0, :, :PART] = pltpu.matmul_pop(acc)[:SLOTS]
-
-    def prepare(m, staging, r, base):
-        pltpu.matmul_push_rhs(right(where_, weigh, r), staging_register=staging, mxu_index=m, transpose=True)
-        ahead[m] = left(place, r, base)
-
-    def multiply(targets, begin, trips, base, then):
+class Bins:
+    def __init__(self, place, where_, weigh, spare, fact, running, ahead, own, unused, accs):
+        self.refs = place, where_, weigh
+        self.spare, self.fact, self.running, self.ahead, self.own, self.unused = spare, fact, running, ahead, own, unused
+        self.accs = accs
+        self.windows = running.shape[0]
+        self.height = (place.shape[0] - SUB) // self.windows
+        self.cuts = splits(self.height)
+        self.order = [(w, p) for p in range(3) for w in range(self.windows)]
+        for acc in accs:
+            unused[:, :PART] = pltpu.matmul_pop(acc)[: unused.shape[0]]
+        for m in range(2):
+            self.push(m, 0, self.start(0) + 2 * m)
+            ahead[m] = left(place, self.start(0) + 2 * m, jnp.float32(0.0))
+
+    def start(self, k):
+        w, p = self.order[k % len(self.order)]
+        return w * self.height + self.cuts[p]
+
+    def push(self, m, staging, r):
+        pltpu.matmul_push_rhs(right(*self.refs[1:], r), staging_register=staging, mxu_index=m, transpose=True)
+
+    def region(self, w, p):
+        at = 2 * (w + self.windows * (p % 2))
+        return self.accs[at : at + 2]
+
+    def multiply(self, w, p):
+        k = self.order.index((w, p))
+        trips = (self.cuts[p + 1] - self.cuts[p]) // STEP
+        base, then = 128.0 * p, 128.0 * self.order[(k + 1) % len(self.order)][1]
+
         def body(i, carry):
             for u in range(UNROLL):
                 m, s = u % 2, u // 2 % 2
-                r = begin + i * STEP + 2 * u
-                pltpu.matmul_push_rhs(
-                    right(where_, weigh, r + 4), staging_register=1 - s, mxu_index=m, transpose=True
-                )
-                pltpu.matmul_acc_lhs(targets[m], ahead[m] if u < 2 else left(place, r, base), load_staged_rhs=s)
-                if u >= UNROLL - 2:
-                    ahead[m] = left(place, r + 4, jnp.where(i == trips - 1, then, base))
+                r = self.start(k) + i * STEP + 2 * u
+                ending = u >= UNROLL - 2
+                later = jnp.where(i == trips - 1, self.start(k + 1) + 2 * m, r + 4) if ending else r + 4
+                self.push(m, 1 - s, later)
+                hot_left = self.ahead[m] if u < 2 else left(self.refs[0], r, base)
+                pltpu.matmul_acc_lhs(self.region(w, p)[m], hot_left, load_staged_rhs=s)
+                if ending:
+                    self.ahead[m] = left(self.refs[0], later, jnp.where(i == trips - 1, then, base))
             return carry
 
         lax.fori_loop(0, trips, body, 0)
 
-    def gather(w, phase, add):
-        got = pltpu.matmul_pop(accs[2 * phase]) + pltpu.matmul_pop(accs[2 * phase + 1])
-        for at, across_, channel, piece in blocks(got, phase):
-            if add:
-                running[w, at, across_] += piece
-                continue
-            piece = piece + spare[w, at, across_]
+    def pop(self, w, p):
+        first, second = self.region(w, p)
+        got = pltpu.matmul_pop(first) + pltpu.matmul_pop(second)
+        return [got[32 * b : 32 * b + 32] for b in range(8)]
+
+    def settle(self, part, w, pieces):
+        for b, piece in enumerate(pieces):
+            j, c = b // 2, b % 2
+            channel = 2 * part + c
+            at, wide = slice(ROWS * channel, ROWS * channel + ROWS), slice(PART * j, PART * j + PART)
+            piece = piece + self.spare[w, at, wide]
             if w:
-                row = fact[w, IMAGE_LAYERS + channel : IMAGE_LAYERS + channel + 1, :]
-                piece = jnp.concatenate([row] * (PART // LANES), axis=1) * running[w - 1, at, across_] + piece
-            running[w, at, across_] = piece
-
-    for m in range(2):
-        prepare(m, 0, 2 * m, jnp.float32(0.0))
-    for w in range(windows):
-        for p in range(3):
-            trips = (cuts[p + 1] - cuts[p]) // STEP
-            multiply(
-                accs[2 * p : 2 * p + 2], w * height + cuts[p], trips,
-                jnp.float32(128.0 * p), jnp.float32(128.0 * ((p + 1) % 3)),
-            )
-        for p in (0, 2, 1):
-            gather(w, p, p == 1)
-    for m in range(2):
-        pltpu.matmul_acc_lhs(accs[m], jnp.zeros((256, 256), jnp.bfloat16), load_staged_rhs=0)
-    running[0, :1, :PART] += (pltpu.matmul_pop(accs[0]) + pltpu.matmul_pop(accs[1]))[:1]
-
-
-def scan_kernel(
-    n, size, place, where_, weigh, spare, fact_ref, running_hbm, out_ref,
+                row = self.fact[w, IMAGE_LAYERS + channel : IMAGE_LAYERS + channel + 1, :]
+                piece = jnp.concatenate([row] * (PART // LANES), axis=1) * self.running[w - 1, at, wide] + piece
+            self.running[w, at, wide] = piece
+            if w == self.windows - 1:
+                per = CHUNK // PART
+                down = c * (COLS // CHUNK) * ROWS + j // per * ROWS
+                self.own[part, down : down + ROWS, j % per * PART : (j % per + 1) * PART] = piece
+
+    def settle_first(self):
+        for w in range(self.windows):
+            outer, inner = self.pop(w, 0), self.pop(w, 1)
+            self.settle(0, w, outer[:4] + [x + y for x, y in zip(outer[4:], inner[:4])])
+            for b, piece in enumerate(inner[4:]):
+                at = (2 + b % 2) * ROWS
+                self.running[w, at : at + ROWS, b // 2 * PART : (b // 2 + 1) * PART] = piece
+
+    def settle_second(self):
+        for w in range(self.windows):
+            pieces = self.pop(w, 2)
+            for b in range(4):
+                at = (2 + b % 2) * ROWS
+                pieces[b] = pieces[b] + self.running[w, at : at + ROWS, b // 2 * PART : (b // 2 + 1) * PART]
+            self.settle(1, w, pieces)
+
+    def close(self):
+        for m in range(2):
+            pltpu.matmul_acc_lhs(self.accs[m], jnp.zeros((256, 256), jnp.bfloat16), load_staged_rhs=0)
+            self.unused[:, :PART] = pltpu.matmul_pop(self.accs[m])[: self.unused.shape[0]]
+
+
+def scan_kernel(n, size, *refs):
+    windows = refs[5].shape[0]
+    pl.run_scoped(
+        lambda *accs: scan(n, size, accs, *refs),
+        *[pltpu.ACC(m)((256, PART), jnp.float32) for _ in range(2 * windows) for m in range(2)],
+    )
+
+
+def scan(
+    n, size, accs, place, where_, weigh, spare, fact_ref, running_ref, out_ref,
     ahead, own, other, stage, inbox, total, earlier, carried, spread, back, prefix, handed, received,
-    load_sem, swap_send, swap_recv, go_send, go_recv, up_send, up_recv, back_send, back_recv, hand_send, hand_recv,
+    swap_send, swap_recv, go_send, go_recv, up_send, up_recv, back_send, back_recv, hand_send, hand_recv,
 ):
-    windows = running_hbm.shape[0]
+    windows = running_ref.shape[0]
     groups, chips = n // size, size // 2
-    half = SLOTS // 2
+    half = COLS // CHUNK * ROWS
     piece = half // chips
-    chunks = COLS // CHUNK
+    chunks = IMAGE_LAYERS // 2
     me = lax.axis_index("win")
     group, member = lax.div(me, size), lax.rem(me, size)
     chip, side = lax.div(member, 2), lax.rem(member, 2)
@@ -255,18 +297,11 @@
     peers = [partner] + [mate(k) for k in range(1, chips)] + [counter(k) for k in range(1, groups)]
     for peer in peers:
         pl.semaphore_signal(barrier, inc=1, device_id=(peer,), device_id_type=MESH)
-    pl.run_scoped(
-        functools.partial(bin_points, place, where_, weigh, spare, fact_ref, running_hbm, ahead),
-        *[pltpu.ACC(m)((256, 256), jnp.float32) for _ in range(3) for m in range(2)],
-    )
-    for c in range(chunks):
-        own[c, :, :CHUNK] = running_hbm[windows - 1, :, c * CHUNK : (c + 1) * CHUNK]
     for channel in range(IMAGE_LAYERS):
         factor = fact_ref[windows - 1, channel : channel + 1, :]
-        own[0, channel * ROWS : (channel + 1) * ROWS, CHUNK:] = jnp.broadcast_to(factor, (ROWS, LANES))
-
-    def sent(ref, chunk):
-        return ref if chunk == 0 else ref.at[:, pl.ds(0, CHUNK)]
+        down = channel % 2 * half
+        own[channel // 2, down : down + half, CHUNK:] = jnp.broadcast_to(factor, (half, LANES))
+    bins = Bins(place, where_, weigh, spare, fact_ref, running_ref, ahead, own, carried, accs)
 
     def remote(src, dst, send, recv, device):
         return pltpu.make_async_remote_copy(
@@ -276,20 +311,20 @@
     def swap_sides(chunk):
         away = own.at[chunk, pl.ds(pl.multiple_of((1 - side) * half, half), half)]
         return remote(
-            sent(away, chunk), sent(other.at[chunk], chunk), swap_send.at[chunk], swap_recv.at[chunk], partner
+            away, other.at[chunk], swap_send.at[chunk], swap_recv.at[chunk], partner
         )
 
     def go(chunk, k, sender):
         peer = lax.rem(chip + k, chips)
         slot = chip if sender else peer
         return remote(
-            sent(stage.at[chunk, peer], chunk), sent(inbox.at[chunk, slot], chunk),
+            stage.at[chunk, peer], inbox.at[chunk, slot],
             go_send.at[chunk, k], go_recv.at[chunk, slot], mate(k),
         )
 
     def up(chunk, k, slot):
         return remote(
-            sent(total.at[chunk], chunk), sent(earlier.at[chunk, slot], chunk),
+            total.at[chunk], earlier.at[chunk, slot],
             up_send.at[chunk, k], up_recv.at[chunk, slot], counter(k),
         )
 
@@ -311,17 +346,15 @@
     def combine(chunk):
         swap_sides(chunk).wait_recv()
         a, b = own[chunk, mine_at, :CHUNK], other[chunk, :, :CHUNK]
-        fa, fb = own[0, mine_at, CHUNK:], other[0, :, CHUNK:]
+        fa, fb = own[chunk, mine_at, CHUNK:], other[chunk, :, CHUNK:]
         late = across(jnp.where(first, fb, fa))
         both = late * jnp.where(first, a, b) + jnp.where(first, b, a)
         for p in range(chips):
             stage[chunk, p, :, :CHUNK] = both[p * piece : (p + 1) * piece]
-            if chunk == 0:
-                stage[chunk, p, :, CHUNK:] = (fa * fb)[p * piece : (p + 1) * piece]
+            stage[chunk, p, :, CHUNK:] = (fa * fb)[p * piece : (p + 1) * piece]
         for k in range(1, chips):
             go(chunk, k, True).start()
-        wide = CHUNK if chunk else CHUNK + LANES
-        inbox[chunk, chip, :, :wide] = stage[chunk, chip, :, :wide]
+        inbox[chunk, chip] = stage[chunk, chip]
 
     def give_all(chunk):
         for k in range(1, chips):
@@ -335,15 +368,12 @@
         factor = jnp.ones((piece, LANES), jnp.float32)
         for m in range(chips):
             back[chunk, m] = running
-            by = inbox[0, m, :, CHUNK:]
-            if chunk == 0:
-                spread[m] = factor
+            by = inbox[chunk, m, :, CHUNK:]
+            spread[chunk, m] = factor
             running = across(by) * running + inbox[chunk, m, :, :CHUNK]
-            if chunk == 0:
-                factor = factor * by
+            factor = factor * by
         total[chunk, :, :CHUNK] = running
-        if chunk == 0:
-            total[chunk, :, CHUNK:] = factor
+        total[chunk, :, CHUNK:] = factor
         for k in range(1, groups):
 
             @pl.when(group + k < groups)
@@ -363,38 +393,50 @@
             @pl.when(g < group)
             def _():
                 up(chunk, 1, g).wait_recv()
-                by = earlier[0, g, :, CHUNK:]
+                by = earlier[chunk, g, :, CHUNK:]
                 carried[...] = across(by) * carried[...] + earlier[chunk, g, :, :CHUNK]
 
         @pl.when(group > 0)
         def _():
             before = carried[...]
             for m in range(chips):
-                back[chunk, m] += across(spread[m]) * before
+                back[chunk, m] += across(spread[chunk, m]) * before
             give_all(chunk)
+
+    def write(chunk, which, values):
+        at = pl.ds(pl.multiple_of((2 * chunk + which) * ROWS, ROWS), ROWS)
+        for j in range(COLS // CHUNK):
+            out_ref[at, j * CHUNK : (j + 1) * CHUNK] = values[j * ROWS : (j + 1) * ROWS]
 
     def pass_on(chunk):
         for k in range(1, chips):
             give(chunk, k, False).wait_recv()
         before = prefix[chunk].reshape(half, CHUNK)
         a, b = own[chunk, mine_at, :CHUNK], other[chunk, :, :CHUNK]
-        fa, fb = own[0, mine_at, CHUNK:], other[0, :, CHUNK:]
+        fa, fb = own[chunk, mine_at, CHUNK:], other[chunk, :, CHUNK:]
         after = across(jnp.where(first, fa, fb)) * before + jnp.where(first, a, b)
         handed[chunk] = jnp.where(first, after, before)
         hand(chunk).start()
-        out_ref[mine_at, chunk * CHUNK : (chunk + 1) * CHUNK] = jnp.where(first, before, after)
+        write(chunk, side, jnp.where(first, before, after))
 
     def take(chunk):
         hand(chunk).wait_recv()
-        at = pl.ds(pl.multiple_of((1 - side) * half, half), half)
-        out_ref[at, chunk * CHUNK : (chunk + 1) * CHUNK] = received[chunk]
-
-    for chunk in range(chunks):
-        if chunk == 0:
-            pl.semaphore_wait(barrier, len(peers))
-        swap_sides(chunk).start()
-    for chunk in range(chunks):
-        combine(chunk)
+        write(chunk, 1 - side, received[chunk])
+
+    for p in range(2):
+        for w in range(windows):
+            bins.multiply(w, p)
+    bins.settle_first()
+    pl.semaphore_wait(barrier, len(peers))
+    swap_sides(0).start()
+    for w in range(windows):
+        if w == windows - 1:
+            combine(0)
+        bins.multiply(w, 2)
+    bins.settle_second()
+    swap_sides(1).start()
+    bins.close()
+    combine(1)
     for chunk in range(chunks):
         scan_group(chunk)
     for chunk in range(chunks):
@@ -421,8 +463,8 @@
     windows = spare.shape[0]
     size = max(s for s in range(2, 2 * SLOTS // (2 * SUB) + 1, 2) if n % s == 0 and SLOTS % (s * SUB) == 0)
     groups, chips = n // size, size // 2
-    half = SLOTS // 2
-    piece, chunks = half // chips, COLS // CHUNK
+    half, chunks = COLS // CHUNK * ROWS, IMAGE_LAYERS // 2
+    piece = half // chips
     wide = CHUNK + LANES
     dma = pltpu.SemaphoreType.DMA
     f32 = lambda *shape: pltpu.VMEM(shape, jnp.float32)
@@ -436,11 +478,11 @@
         out_specs=[pl.BlockSpec(memory_space=pltpu.VMEM)] * 2,
         scratch_shapes=[
             pltpu.VMEM((2, 256, 256), jnp.bfloat16),
-            f32(chunks, SLOTS, wide), f32(chunks, half, wide), f32(chunks, chips, piece, wide),
+            f32(chunks, 2 * half, wide), f32(chunks, half, wide), f32(chunks, chips, piece, wide),
             f32(chunks, chips, piece, wide), f32(chunks, piece, wide), f32(chunks, groups, piece, wide),
-            f32(piece, CHUNK), f32(chips, piece, LANES), f32(chunks, chips, piece, CHUNK),
+            f32(piece, CHUNK), f32(chunks, chips, piece, LANES), f32(chunks, chips, piece, CHUNK),
             f32(chunks, chips, piece, CHUNK), f32(chunks, half, CHUNK), f32(chunks, half, CHUNK),
-            dma((chunks,)), dma((chunks,)), dma((chunks,)), dma((chunks, chips)), dma((chunks, chips)),
+            dma((chunks,)), dma((chunks,)), dma((chunks, chips)), dma((chunks, chips)),
             dma((chunks, groups)), dma((chunks, groups)), dma((chunks, chips)), dma((chunks, chips)),
             dma((chunks,)), dma((chunks,)),
         ],

time: 31.2 us -> 29.8 us (0.955)
  Pallas kernels: 31.1 us -> 29.6 us
    pallas_call x1, Pallas kernels: 26.9 us -> 25.4 us  [before_own(): pl.pallas_call(functools.partial(scan_kernel, n, size), out_shape=(jax.Sh...]
where the time goes in v4:
time: 29.8 us; the launch traced here: 29.7 us
  Pallas kernels  29.6 us (99%)
    pallas_call x1, Pallas kernels, before_own(): pl.pallas_call(functools.partial(scan_kernel, n, size), out_shape=(jax.Sh...  25.4 us
    pallas_call x1, Pallas kernels, binned(): pl.pallas_call(kernel, out_shape=(points, points, points, jax.ShapeDtypeS...  3.16 us
    pallas_call x1, Pallas kernels, heat(): pl.pallas_call(heat_kernel, out_shape=jax.ShapeDtypeStruct(running.shape,...  1.04 us

profile of v4, /device:TPU:17, one launch (start us, length us, event | category | flops | bytes accessed | tf_op | source)
XLA Modules:
  0.0 29.7 jit_solution(5162990493632159034)
XLA Ops:
  0.0 3.2 %shard_map.55 = (f32[520,128]{1,0:T(8,128)S(1)}, f32[520,128]{1,0:T(8,128)S(1)}, f32[520,128]{1,0:T(8,128)S(1)}, f32[2,128,1024]{2,1,0:T(8,128)S(1)}, f32[2,8,128]{2,1,0:T(8,128)S(1)}) custom-call(s32[512,128]{1,0:T(8,128)} %bitcast.21, s32[512,128]{1,0:T(8,128)} %bitcast.22, s32[512,128]{1,0:T(8,128)} %bitcast.23, bf16[512,128]{1,0:T(8,128)(2,1)} %bitcast.24, ...), custom_call_target="tpu_custom_call" | custom-call | tf_op jit(solution)/shard_map/pallas_call | solution.py:158
  3.2 25.4 %shard_map.56 = (f32[2,128,1024]{2,1,0:T(8,128)S(1)}, f32[128,1024]{1,0:T(8,128)S(1)}) custom-call(f32[520,128]{1,0:T(8,128)S(1)} %get-tuple-element.12.refs_0_, f32[520,128]{1,0:T(8,128)S(1)} %get-tuple-element.13.refs_1_, f32[520,128]{1,0:T(8,128)S(1)} %get-tuple-element.14.refs_2_, f32[2,128,1024]{2,1,0:T(8,128)S(1)} %get-tuple-element.15.refs_3_, ...), custom_call_target="tpu_custom_call" | custom-call | tf_op jit(solution)/shard_map/pallas_call | solution.py:471
  28.6 1.0 %shard_map.57 = f32[2,128,1024]{2,1,0:T(8,128)} custom-call(f32[2,128,1024]{2,1,0:T(8,128)S(1)} %get-tuple-element.17.running_ref, f32[128,1024]{1,0:T(8,128)S(1)} %get-tuple-element.18.before_ref, f32[2,8,128]{2,1,0:T(8,128)S(1)} %get-tuple-element.16.refs_4_.fact_ref), custom_call_target="tpu_custom_call" | custom-call | tf_op jit(solution)/shard_map/pallas_call | solution.py:511

commit v5 on v4

--- a/solution.py
+++ b/solution.py
@@ -7,7 +7,7 @@
 IMAGE_LAYERS=4
 SLOTS=128; ROWS=32; COLS=1024; PART=256; LANES=128; SUB=8
 PARTS=2
-UNROLL=8
+UNROLL=16
 STEP=2*UNROLL
 def hot(index, on):
     spread = jnp.broadcast_to(index, (16, LANES)).astype(jnp.bfloat16)

time: 29.8 us -> 29.2 us (0.980)
  Pallas kernels: 29.6 us -> 29.1 us
    pallas_call x1, Pallas kernels: 25.4 us -> 24.9 us  [before_own(): pl.pallas_call(functools.partial(scan_kernel, n, size), out_shape=(jax.Sh...]
where the time goes in v5:
time: 29.2 us; the launch traced here: 29.1 us
  Pallas kernels  29.1 us (100%)
    pallas_call x1, Pallas kernels, before_own(): pl.pallas_call(functools.partial(scan_kernel, n, size), out_shape=(jax.Sh...  24.9 us
    pallas_call x1, Pallas kernels, binned(): pl.pallas_call(kernel, out_shape=(points, points, points, jax.ShapeDtypeS...  3.16 us
    pallas_call x1, Pallas kernels, heat(): pl.pallas_call(heat_kernel, out_shape=jax.ShapeDtypeStruct(running.shape,...  1.04 us

profile of v5, /device:TPU:17, one launch (start us, length us, event | category | flops | bytes accessed | tf_op | source)
XLA Modules:
  0.0 29.1 jit_solution(10231981469954824779)
XLA Ops:
  0.0 3.2 %shard_map.55 = (f32[520,128]{1,0:T(8,128)S(1)}, f32[520,128]{1,0:T(8,128)S(1)}, f32[520,128]{1,0:T(8,128)S(1)}, f32[2,128,1024]{2,1,0:T(8,128)S(1)}, f32[2,8,128]{2,1,0:T(8,128)S(1)}) custom-call(s32[512,128]{1,0:T(8,128)} %bitcast.21, s32[512,128]{1,0:T(8,128)} %bitcast.22, s32[512,128]{1,0:T(8,128)} %bitcast.23, bf16[512,128]{1,0:T(8,128)(2,1)} %bitcast.24, ...), custom_call_target="tpu_custom_call" | custom-call | tf_op jit(solution)/shard_map/pallas_call | solution.py:158
  3.2 24.9 %shard_map.56 = (f32[2,128,1024]{2,1,0:T(8,128)S(1)}, f32[128,1024]{1,0:T(8,128)S(1)}) custom-call(f32[520,128]{1,0:T(8,128)S(1)} %get-tuple-element.12.refs_0_, f32[520,128]{1,0:T(8,128)S(1)} %get-tuple-element.13.refs_1_, f32[520,128]{1,0:T(8,128)S(1)} %get-tuple-element.14.refs_2_, f32[2,128,1024]{2,1,0:T(8,128)S(1)} %get-tuple-element.15.refs_3_, ...), custom_call_target="tpu_custom_call" | custom-call | tf_op jit(solution)/shard_map/pallas_call | solution.py:471
  28.0 1.0 %shard_map.57 = f32[2,128,1024]{2,1,0:T(8,128)} custom-call(f32[2,128,1024]{2,1,0:T(8,128)S(1)} %get-tuple-element.17.running_ref, f32[128,1024]{1,0:T(8,128)S(1)} %get-tuple-element.18.before_ref, f32[2,8,128]{2,1,0:T(8,128)S(1)} %get-tuple-element.16.refs_4_.fact_ref), custom_call_target="tpu_custom_call" | custom-call | tf_op jit(solution)/shard_map/pallas_call | solution.py:511

commit v6 on v5

--- a/solution.py
+++ b/solution.py
@@ -399,9 +399,11 @@
         @pl.when(group > 0)
         def _():
             before = carried[...]
-            for m in range(chips):
-                back[chunk, m] += across(spread[chunk, m]) * before
-            give_all(chunk)
+            for k in range(1, chips):
+                peer = lax.rem(chip + k, chips)
+                back[chunk, peer] += across(spread[chunk, peer]) * before
+                give(chunk, k, True).start()
+            prefix[chunk, chip] = back[chunk, chip] + across(spread[chunk, chip]) * before
 
     def write(chunk, which, values):
         at = pl.ds(pl.multiple_of((2 * chunk + which) * ROWS, ROWS), ROWS)
@@ -439,7 +441,9 @@
     combine(1)
     for chunk in range(chunks):
         scan_group(chunk)
-    for chunk in range(chunks):
+        if chunk == 0:
+            finish_groups(chunk)
+    for chunk in range(1, chunks):
         finish_groups(chunk)
     for chunk in range(chunks):
         pass_on(chunk)

time: 29.2 us -> 29.3 us (level)
  no operation moved by 1% of the time
where the time goes in v6:
time: 29.3 us; the launch traced here: 29.1 us
  Pallas kernels  29.1 us (99%)
    pallas_call x1, Pallas kernels, before_own(): pl.pallas_call(functools.partial(scan_kernel, n, size), out_shape=(jax.Sh...  24.9 us
    pallas_call x1, Pallas kernels, binned(): pl.pallas_call(kernel, out_shape=(points, points, points, jax.ShapeDtypeS...  3.16 us
    pallas_call x1, Pallas kernels, heat(): pl.pallas_call(heat_kernel, out_shape=jax.ShapeDtypeStruct(running.shape,...  1.04 us

profile of v6, /device:TPU:17, one launch (start us, length us, event | category | flops | bytes accessed | tf_op | source)
XLA Modules:
  0.0 29.1 jit_solution(5839164666474590309)
XLA Ops:
  0.0 3.2 %shard_map.55 = (f32[520,128]{1,0:T(8,128)S(1)}, f32[520,128]{1,0:T(8,128)S(1)}, f32[520,128]{1,0:T(8,128)S(1)}, f32[2,128,1024]{2,1,0:T(8,128)S(1)}, f32[2,8,128]{2,1,0:T(8,128)S(1)}) custom-call(s32[512,128]{1,0:T(8,128)} %bitcast.21, s32[512,128]{1,0:T(8,128)} %bitcast.22, s32[512,128]{1,0:T(8,128)} %bitcast.23, bf16[512,128]{1,0:T(8,128)(2,1)} %bitcast.24, ...), custom_call_target="tpu_custom_call" | custom-call | tf_op jit(solution)/shard_map/pallas_call | solution.py:158
  3.2 24.9 %shard_map.56 = (f32[2,128,1024]{2,1,0:T(8,128)S(1)}, f32[128,1024]{1,0:T(8,128)S(1)}) custom-call(f32[520,128]{1,0:T(8,128)S(1)} %get-tuple-element.12.refs_0_, f32[520,128]{1,0:T(8,128)S(1)} %get-tuple-element.13.refs_1_, f32[520,128]{1,0:T(8,128)S(1)} %get-tuple-element.14.refs_2_, f32[2,128,1024]{2,1,0:T(8,128)S(1)} %get-tuple-element.15.refs_3_, ...), custom_call_target="tpu_custom_call" | custom-call | tf_op jit(solution)/shard_map/pallas_call | solution.py:475
  28.1 1.0 %shard_map.57 = f32[2,128,1024]{2,1,0:T(8,128)} custom-call(f32[2,128,1024]{2,1,0:T(8,128)S(1)} %get-tuple-element.17.running_ref, f32[128,1024]{1,0:T(8,128)S(1)} %get-tuple-element.18.before_ref, f32[2,8,128]{2,1,0:T(8,128)S(1)} %get-tuple-element.16.refs_4_.fact_ref), custom_call_target="tpu_custom_call" | custom-call | tf_op jit(solution)/shard_map/pallas_call | solution.py:515
